TPU v7x, 32 devices: a whole 2x2x4 slice. The times are simulated.
32 devices in a mesh: ta: 4 (over y, x), gy: 2 (over core), gx: 4 (over z).
Axes of the slice: x: 2, y: 2, z: 4, core: 2. Of those that a mesh axis runs over, the one named last changes fastest.
Arguments:
- features: bfloat16 [16, 4, 416, 192], P('ta', 'gy', 'gx'), may hold values from -6 to 6
- gain_first: float32 [192], replicated, may hold values from 0.1 to 1.9
- kernel_first: bfloat16 [3, 3, 3, 192, 192], replicated, may hold values from -0.078125 to 0.078125
- bias_first: float32 [192], replicated, may hold values from -3 to 3
- gain_second: float32 [192], replicated, may hold values from 0.1 to 1.9
- kernel_second: bfloat16 [3, 3, 3, 192, 192], replicated, may hold values from -0.078125 to 0.078125
- bias_second: float32 [192], replicated, may hold values from -3 to 3
Outputs:
- block_out: bfloat16 [16, 4, 416, 192], P('ta', 'gy', 'gx')
All inputs are finite; a program needn't handle non-finite values.
Results may differ from a plain program's by a relative error of at most 0.0075.
Values may be sent and summed in bfloat16 or wider, within the bound.
A program may use at most 64 MiB of HBM per device.

v0:
```python
import functools

import jax
import jax.numpy as jnp
from jax import lax
from jax.experimental import pallas as pl
from jax.experimental.pallas import tpu as pltpu
from jax.sharding import PartitionSpec as P

epsilon = 1e-06
LATE, EARLY, PAST = 0, 1, 2
MOVES = [(dy, dx) for dy in (-1, 0, 1) for dx in (-1, 0, 1)]


def moves_of(kind):
    return [m for m in MOVES if kind == PAST or m != (0, 0)]


def activate(field, gain):
    meansq = jnp.mean(field * field, axis=-1, keepdims=True)
    u = field * lax.rsqrt(meansq + epsilon) * gain
    return u / (1.0 + jnp.exp(-u))


def block_kernel(
    feat, gain1, bias1, gain2, bias2, k1, k2, out,
    weights, act, edges, main_in, row_in, edge_in, line, cols3, acc,
    w_sem, send_sem, recv_sem,
):
    rows, cols, ch = feat.shape[1:]
    colsp = acc.shape[0] // (2 * rows)
    lanes = line.shape[-1]
    ta, gy, gx = (lax.axis_index(a) for a in ("ta", "gy", "gx"))
    n_ta, n_gy, n_gx = (lax.axis_size(a) for a in ("ta", "gy", "gx"))

    def inside(kind, dy, dx, sign):
        t = ta + sign * (1 if kind == PAST else 0)
        y, x = gy + sign * dy, gx + sign * dx
        ok = (t >= 0) & (t < n_ta) & (y >= 0) & (y < n_gy) & (x >= 0) & (x < n_gx)
        return ok, {"ta": t, "gy": y, "gx": x}

    w_copies = [
        pltpu.make_async_copy(k, weights.at[layer, :, pl.ds(0, ch)], w_sem.at[layer])
        for layer, k in enumerate((k1, k2))
    ]
    w_copies[0].start()
    w_copies[1].start()

    barrier = pltpu.get_barrier_semaphore()
    expected = jnp.int32(0)
    for kind in (LATE, PAST):
        for dy, dx in moves_of(kind):
            ok, source = inside(kind, dy, dx, -1)

            @pl.when(ok)
            def _():
                pl.semaphore_signal(
                    barrier, inc=1, device_id=source, device_id_type=pl.DeviceIdType.MESH
                )

            expected = expected + inside(kind, dy, dx, 1)[0].astype(jnp.int32)

    def landing(layer, kind, dy, dx):
        if dx:
            return edge_in.at[layer, kind, dy + 1, (dx + 1) // 2]
        if dy:
            return row_in.at[layer, kind, (dy + 1) // 2]
        return main_in.at[layer]

    def copy_of(layer, kind, dy, dx):
        half = EARLY if kind == EARLY else LATE
        frame = 0 if kind == EARLY else 2
        if dx:
            src = edges.at[layer, half, (dx + 1) // 2]
        elif dy:
            src = act.at[layer, pl.ds(frame, 2), rows - 1 if dy > 0 else 0]
        else:
            src = act.at[layer, pl.ds(frame, 2)]
        number = kind * 9 + (dy + 1) * 3 + dx + 1
        ok, target = inside(kind, dy, dx, 1)
        return ok, pltpu.make_async_remote_copy(
            src_ref=src,
            dst_ref=landing(layer, kind, dy, dx),
            send_sem=send_sem.at[layer, number],
            recv_sem=recv_sem.at[layer, number],
            device_id=target,
            device_id_type=pl.DeviceIdType.MESH,
        )

    def send(layer, kind):
        for dy, dx in sorted(moves_of(kind), key=lambda m: (m[1] != 0, m)):
            ok, copy = copy_of(layer, kind, dy, dx)
            pl.when(ok)(copy.start)

    def receive(layer, kind):
        for dy, dx in moves_of(kind):
            ok, _ = inside(kind, dy, dx, -1)
            copy = copy_of(layer, kind, dy, dx)[1]
            place = landing(layer, kind, dy, dx)
            pl.when(ok)(copy.wait_recv)

            @pl.when(jnp.logical_not(ok))
            def _():
                place[...] = jnp.zeros_like(place)

    def keep(layer, frame, row, value):
        half = LATE if frame >= 2 else EARLY
        act[layer, frame, row] = value.astype(jnp.bfloat16)
        value = value.astype(jnp.bfloat16).astype(jnp.float32)
        at = (frame % 2) * rows + row
        edges[layer, half, 0, at : at + 1, :] = value[0:1]
        edges[layer, half, 1, at : at + 1, :] = value[cols - 1 : cols]

    def spread(layer, kind):
        base = {LATE: 4, EARLY: 2, PAST: 0}[kind]
        for f in range(2):
            for row in range(-1, rows + 1):
                if row < 0 or row >= rows:
                    dy = 1 if row < 0 else -1
                    source = row_in[layer, kind, (dy + 1) // 2, f]
                    at = f * rows + (rows - 1 if row < 0 else 0)
                else:
                    dy = 0
                    at = f * rows + row
                    if kind == PAST:
                        source = main_in[layer, f, row]
                    else:
                        source = act[layer, base - 2 + f, row]
                slot = f * (rows + 2) + row + 1
                line[slot, 8 : 8 + cols, 0:ch] = source.astype(jnp.float32)
                line[slot, 7:8, 0:ch] = edge_in[layer, kind, dy + 1, 1, at : at + 1, :]
                line[slot, 8 + cols : 9 + cols, 0:ch] = edge_in[layer, kind, dy + 1, 0, at : at + 1, :]
                for r in range(3):
                    cols3[layer, base + f, row + 1, 0:cols, r * lanes : (r + 1) * lanes] = line[
                        slot, 7 + r : 7 + r + cols, :
                    ].astype(jnp.bfloat16)

    def convolve(layer, frame):
        def tap(p, _):
            total = None
            for q in range(3):
                piece = cols3[layer, pl.ds(frame + p, 2), q : q + rows].reshape(-1, 3 * lanes)
                kernel = weights[layer, pl.ds(9 * p + 3 * q, 3)].reshape(3 * lanes, ch)
                part = jnp.dot(piece, kernel, preferred_element_type=jnp.float32)
                total = part if total is None else total + part
            acc[...] += total
            return 0

        acc[...] = jnp.zeros_like(acc)
        lax.fori_loop(0, 3, tap, 0)

    def cells(f, row):
        at = (f * rows + row) * colsp
        return acc[at : at + cols, :]

    def middle(frame):
        for f in range(2):
            for row in range(rows):
                value = (cells(f, row) + bias1[...]).astype(jnp.bfloat16).astype(jnp.float32)
                keep(1, frame + f, row, activate(value, gain2[...]))

    def finish(frame):
        for f in range(2):
            for row in range(rows):
                value = cells(f, row) + bias2[...] + feat[frame + f, row].astype(jnp.float32)
                out[frame + f, row] = value.astype(jnp.bfloat16)

    def first(frame):
        for f in range(2):
            for row in range(rows):
                keep(0, frame + f, row, activate(feat[frame + f, row].astype(jnp.float32), gain1[...]))

    edges[...] = jnp.zeros_like(edges)
    first(2)
    pl.semaphore_wait(barrier, expected)
    send(0, PAST)
    send(0, LATE)
    first(0)
    send(0, EARLY)
    weights[:, :, ch:, :] = jnp.zeros((2, weights.shape[1], lanes - ch, ch), jnp.bfloat16)
    line[...] = jnp.zeros_like(line)
    receive(0, LATE)
    spread(0, LATE)
    receive(0, EARLY)
    spread(0, EARLY)
    w_copies[0].wait()
    convolve(0, 2)
    middle(2)
    send(1, PAST)
    send(1, LATE)
    receive(0, PAST)
    spread(0, PAST)
    convolve(0, 0)
    middle(0)
    send(1, EARLY)
    receive(1, LATE)
    spread(1, LATE)
    receive(1, EARLY)
    spread(1, EARLY)
    w_copies[1].wait()
    convolve(1, 2)
    finish(2)
    receive(1, PAST)
    spread(1, PAST)
    convolve(1, 0)
    finish(0)
    for layer in range(2):
        for kind in (LATE, EARLY, PAST):
            for dy, dx in moves_of(kind):
                ok, copy = copy_of(layer, kind, dy, dx)
                pl.when(ok)(copy.wait_send)


def local(features, gain_first, kernel_first, bias_first, gain_second, kernel_second, bias_second):
    frames, rows, cols, ch = features.shape
    colsp = -(-cols // 16) * 16
    lanes = -(-ch // 128) * 128
    vmem = pl.BlockSpec(memory_space=pltpu.VMEM)
    hbm = pl.BlockSpec(memory_space=pl.ANY)
    edge_rows = -(-2 * rows // 8) * 8
    bf16, f32 = jnp.bfloat16, jnp.float32
    return pl.pallas_call(
        block_kernel,
        out_shape=jax.ShapeDtypeStruct(features.shape, bf16),
        in_specs=[vmem] * 5 + [hbm] * 2,
        out_specs=vmem,
        scratch_shapes=[
            pltpu.VMEM((2, 27, lanes, ch), bf16),
            pltpu.VMEM((2, frames, rows, cols, ch), bf16),
            pltpu.VMEM((2, 2, 2, edge_rows, ch), f32),
            pltpu.VMEM((2, 2, rows, cols, ch), bf16),
            pltpu.VMEM((2, 3, 2, 2, cols, ch), bf16),
            pltpu.VMEM((2, 3, 3, 2, edge_rows, ch), f32),
            pltpu.VMEM((2 * (rows + 2), cols + 16, lanes), f32),
            pltpu.VMEM((2, frames + 2, rows + 2, colsp, 3 * lanes), bf16),
            pltpu.VMEM((2 * rows * colsp, ch), f32),
            pltpu.SemaphoreType.DMA((2,)),
            pltpu.SemaphoreType.DMA((2, 27)),
            pltpu.SemaphoreType.DMA((2, 27)),
        ],
        compiler_params=pltpu.CompilerParams(
            collective_id=0, has_side_effects=True, vmem_limit_bytes=56 * 1024 * 1024
        ),
        name="residual_block",
    )(
        features,
        gain_first.reshape(1, ch),
        bias_first.reshape(1, ch),
        gain_second.reshape(1, ch),
        bias_second.reshape(1, ch),
        kernel_first.reshape(27, ch, ch),
        kernel_second.reshape(27, ch, ch),
    )


def solution(mesh):
    placed = (P("ta", "gy", "gx", None), P(), P(), P(), P(), P(), P())
    return jax.shard_map(
        local, mesh=mesh, in_specs=placed, out_specs=P("ta", "gy", "gx", None), check_vma=False
    )
```

profile of v0, /device:TPU:5, one launch (start us, length us, event | category | flops | bytes accessed | tf_op | source)
XLA Modules:
  0.0 30.8 jit_solution(1643813451688630565)
XLA Ops:
  0.0 1.9 %copy.8.feat = bf16[4,2,104,192]{3,2,1,0:T(8,128)(2,1)} copy(bf16[4,2,104,192]{2,3,1,0:T(8,128)(2,1)} %param.7) | data formatting | bytes 638976 | tf_op args[0]
  1.9 26.9 %residual_block.1 = bf16[4,2,104,192]{3,2,1,0:T(8,128)(2,1)} custom-call(bf16[4,2,104,192]{3,2,1,0:T(8,128)(2,1)} %copy.8.feat, f32[1,192]{1,0:T(1,128)} %bitcast.8, f32[1,192]{1,0:T(1,128)} %bitcast.9, f32[1,192]{1,0:T(1,128)} %bitcast.10, f32[1,192]{1,0:T(1,128)} %bitcast.11, bf16[27,192,192]{2,1,0:T(8,128)(2,1)} %bitcast.6, bf16[27,192,192]{2,1,0:T(8,128)(2,1)} %bitcast.7), custom_call_target="tpu_custom_call" | custom-call | tf_op jit(solution)/shard_map/residual_block/pallas_call | solution.py:222
  28.8 2.0 %copy.9 = bf16[4,2,104,192]{2,3,1,0:T(8,128)(2,1)} copy(bf16[4,2,104,192]{3,2,1,0:T(8,128)(2,1)} %residual_block.1) | data formatting | bytes 638976 | tf_op jit(solution)/shard_map/residual_block/pallas_call | solution.py:222
where the time goes:
time: 31 us; the launch traced here: 30.8 us
  Pallas kernels  26.9 us (87%)
  local copies, waits for them, and re-layouts  3.9 us (13%)
    pallas_call x1, Pallas kernels, local(): pl.pallas_call(block_kernel, out_shape=jax.ShapeDtypeStruct(features.shap...  26.9 us
    pallas_call x1, local copies, waits for them, and re-layouts, local(): pl.pallas_call(block_kernel, out_shape=jax.ShapeDtypeStruct(features.shap...  1.95 us
    unnamed x1, local copies, waits for them, and re-layouts  1.95 us

commit v1 on v0

v1 whole, which is shorter than its diff:
```python
import functools

import jax
import jax.numpy as jnp
from jax import lax
from jax.experimental import pallas as pl
from jax.experimental.pallas import tpu as pltpu
from jax.sharding import PartitionSpec as P

epsilon = 1e-06
LATE, EARLY, PAST = 0, 1, 2
TILE = 128
MOVES = [(dy, dx) for dy in (-1, 0, 1) for dx in (-1, 0, 1)]


def moves_of(kind):
    return [m for m in MOVES if kind == PAST or m != (0, 0)]


def activate(field, gain):
    meansq = jnp.mean(field * field, axis=-1, keepdims=True)
    u = field * lax.rsqrt(meansq + epsilon) * gain
    return u / (1.0 + jnp.exp(-u))


def block_kernel(
    feat, gain1, bias1, gain2, bias2, k1, k2, out,
    weights, act, edges, main_in, row_in, edge_in, line, cols3, acc,
    w_sem, send_sem, recv_sem,
):
    rows, cols, ch = feat.shape[1:]
    colsp = acc.shape[1] // (2 * rows)
    lanes = line.shape[-1]
    ta, gy, gx = (lax.axis_index(a) for a in ("ta", "gy", "gx"))
    n_ta, n_gy, n_gx = (lax.axis_size(a) for a in ("ta", "gy", "gx"))

    def inside(kind, dy, dx, sign):
        relayed = kind == PAST and dy != 0 and dx == 0
        t = ta + sign * (1 if kind == PAST and not relayed else 0)
        y, x = gy + sign * dy, gx + sign * dx
        ok = (t >= 0) & (t < n_ta) & (y >= 0) & (y < n_gy) & (x >= 0) & (x < n_gx)
        if relayed:
            ok = ok & (ta > 0)
        return ok, {"ta": t, "gy": y, "gx": x}

    w_copies = [
        pltpu.make_async_copy(k, weights.at[layer, :, pl.ds(0, ch)], w_sem.at[layer])
        for layer, k in enumerate((k1, k2))
    ]
    w_copies[0].start()
    w_copies[1].start()

    barrier = pltpu.get_barrier_semaphore()
    expected = jnp.int32(0)
    for kind in (LATE, PAST):
        for dy, dx in moves_of(kind):
            if kind == PAST and dx == 0 and dy != 0:
                continue
            ok, source = inside(kind, dy, dx, -1)

            @pl.when(ok)
            def _():
                pl.semaphore_signal(
                    barrier, inc=1, device_id=source, device_id_type=pl.DeviceIdType.MESH
                )

            expected = expected + inside(kind, dy, dx, 1)[0].astype(jnp.int32)

    def landing(layer, kind, dy, dx):
        if dx:
            return edge_in.at[layer, kind, dy + 1, (dx + 1) // 2]
        if dy:
            return row_in.at[layer, kind, (dy + 1) // 2]
        return main_in.at[layer]

    def copy_of(layer, kind, dy, dx):
        half = EARLY if kind == EARLY else LATE
        if dx:
            src = edges.at[layer, half, (dx + 1) // 2]
        elif dy:
            edge_row = rows - 1 if dy > 0 else 0
            if kind == PAST:
                src = main_in.at[layer, :, edge_row]
            else:
                src = act.at[layer, half, :, edge_row]
        else:
            src = act.at[layer, LATE]
        number = kind * 9 + (dy + 1) * 3 + dx + 1
        ok, target = inside(kind, dy, dx, 1)
        return ok, pltpu.make_async_remote_copy(
            src_ref=src,
            dst_ref=landing(layer, kind, dy, dx),
            send_sem=send_sem.at[layer, number],
            recv_sem=recv_sem.at[layer, number],
            device_id=target,
            device_id_type=pl.DeviceIdType.MESH,
        )

    def send(layer, moves):
        for kind, dy, dx in moves:
            ok, copy = copy_of(layer, kind, dy, dx)
            pl.when(ok)(copy.start)

    def send_late(layer):
        send(layer, [(LATE, -1, 0), (LATE, 1, 0)])
        send(layer, [(kind, *m) for kind in (LATE, PAST) for m in MOVES if m[1]])
        send(layer, [(PAST, 0, 0)])

    def send_early(layer):
        send(layer, [(EARLY, *m) for m in sorted(moves_of(EARLY), key=lambda m: (m[1] != 0, m))])

    def receive(layer, kind, moves):
        for dy, dx in moves:
            ok, _ = inside(kind, dy, dx, -1)
            copy = copy_of(layer, kind, dy, dx)[1]
            place = landing(layer, kind, dy, dx)
            pl.when(ok)(copy.wait_recv)

            @pl.when(jnp.logical_not(ok))
            def _():
                place[...] = jnp.zeros_like(place)

    def receive_past(layer):
        receive(layer, PAST, [(0, 0)])
        send(layer, [(PAST, -1, 0), (PAST, 1, 0)])
        receive(layer, PAST, [m for m in moves_of(PAST) if m != (0, 0)])

    def keep(layer, half, row, values):
        for f, value in enumerate(values):
            packed = value.astype(jnp.bfloat16)
            act[layer, half, f, row] = packed[:, 0:TILE]
            value = packed.astype(jnp.float32)
            at = f * rows + row
            edges[layer, half, 0, at : at + 1, :] = value[0:1]
            edges[layer, half, 1, at : at + 1, :] = value[cols - 1 : cols]
        tails = jnp.concatenate([value[:, TILE:ch] for value in values], axis=1)
        act[layer, half, 2, row] = tails.astype(jnp.bfloat16)

    def spread(layer, kind):
        base = {LATE: 4, EARLY: 2, PAST: 0}[kind]
        for row in range(-1, rows + 1):
            if row < 0 or row >= rows:
                dy = 1 if row < 0 else -1
                source = row_in.at[layer, kind, (dy + 1) // 2]
                edge_row = rows - 1 if row < 0 else 0
            else:
                dy = 0
                source = main_in.at[layer, :, row] if kind == PAST else act.at[layer, kind, :, row]
                edge_row = row
            tails = source[2].astype(jnp.float32)
            for f in range(2):
                at = f * rows + edge_row
                slot = f * (rows + 2) + row + 1
                line[slot, 8 : 8 + cols, 0:TILE] = source[f].astype(jnp.float32)
                line[slot, 8 : 8 + cols, TILE:lanes] = pltpu.roll(tails, TILE // 2, 1) if f else tails
                line[slot, 7:8, 0:ch] = edge_in[layer, kind, dy + 1, 1, at : at + 1, :]
                line[slot, 8 + cols : 9 + cols, 0:ch] = edge_in[layer, kind, dy + 1, 0, at : at + 1, :]
                for r in range(3):
                    cols3[layer, base + f, row + 1, 0:cols, r * lanes : (r + 1) * lanes] = line[
                        slot, 7 + r : 7 + r + cols, :
                    ].astype(jnp.bfloat16)

    def convolve(layer, frame, own):
        total_at = acc.at[1 if frame else 0]

        def product(p):
            total = None
            for q in range(3):
                piece = cols3[layer, pl.ds(frame + p, 2), q : q + rows].reshape(-1, 3 * lanes)
                kernel = weights[layer, pl.ds(9 * p + 3 * q, 3)].reshape(3 * lanes, ch)
                part = jnp.dot(piece, kernel, preferred_element_type=jnp.float32)
                total = part if total is None else total + part
            return total

        def tap(p, _):
            total_at[...] += product(p)
            return 0

        if own:
            total_at[...] = product(2)
        else:
            lax.fori_loop(0, 2, tap, 0)

    def cells(half, f, row):
        at = (f * rows + row) * colsp
        return acc[1 - half, at : at + cols, :]

    def middle(half):
        for row in range(rows):
            values = []
            for f in range(2):
                value = (cells(half, f, row) + bias1[...]).astype(jnp.bfloat16).astype(jnp.float32)
                values.append(activate(value, gain2[...]))
            keep(1, half, row, values)

    def finish(half):
        frame = 0 if half == EARLY else 2
        for f in range(2):
            for row in range(rows):
                value = cells(half, f, row) + bias2[...] + feat[frame + f, row].astype(jnp.float32)
                out[frame + f, row] = value.astype(jnp.bfloat16)

    def first(half):
        frame = 0 if half == EARLY else 2
        for row in range(rows):
            keep(0, half, row, [
                activate(feat[frame + f, row].astype(jnp.float32), gain1[...]) for f in range(2)
            ])

    edges[...] = jnp.zeros_like(edges)
    first(LATE)
    pl.semaphore_wait(barrier, expected)
    send_late(0)
    first(EARLY)
    send_early(0)
    weights[:, :, ch:, :] = jnp.zeros((2, weights.shape[1], lanes - ch, ch), jnp.bfloat16)
    line[...] = jnp.zeros_like(line)
    receive(0, LATE, moves_of(LATE))
    spread(0, LATE)
    w_copies[0].wait()
    convolve(0, 2, True)
    receive(0, EARLY, moves_of(EARLY))
    spread(0, EARLY)
    convolve(0, 2, False)
    middle(LATE)
    send_late(1)
    convolve(0, 0, True)
    w_copies[1].wait()
    receive(1, LATE, moves_of(LATE))
    spread(1, LATE)
    convolve(1, 2, True)
    receive_past(0)
    spread(0, PAST)
    convolve(0, 0, False)
    middle(EARLY)
    send_early(1)
    receive(1, EARLY, moves_of(EARLY))
    spread(1, EARLY)
    convolve(1, 2, False)
    finish(LATE)
    convolve(1, 0, True)
    receive_past(1)
    spread(1, PAST)
    convolve(1, 0, False)
    finish(EARLY)
    for layer in range(2):
        for kind in (LATE, EARLY, PAST):
            for dy, dx in moves_of(kind):
                ok, copy = copy_of(layer, kind, dy, dx)
                pl.when(ok)(copy.wait_send)


def local(features, gain_first, kernel_first, bias_first, gain_second, kernel_second, bias_second):
    frames, rows, cols, ch = features.shape
    colsp = -(-cols // 16) * 16
    lanes = -(-ch // 128) * 128
    vmem = pl.BlockSpec(memory_space=pltpu.VMEM)
    hbm = pl.BlockSpec(memory_space=pl.ANY)
    edge_rows = -(-2 * rows // 8) * 8
    bf16, f32 = jnp.bfloat16, jnp.float32
    return pl.pallas_call(
        block_kernel,
        out_shape=jax.ShapeDtypeStruct(features.shape, bf16),
        in_specs=[vmem] * 5 + [hbm] * 2,
        out_specs=vmem,
        scratch_shapes=[
            pltpu.VMEM((2, 27, lanes, ch), bf16),
            pltpu.VMEM((2, 2, 3, rows, cols, TILE), bf16),
            pltpu.VMEM((2, 2, 2, edge_rows, ch), f32),
            pltpu.VMEM((2, 3, rows, cols, TILE), bf16),
            pltpu.VMEM((2, 3, 2, 3, cols, TILE), bf16),
            pltpu.VMEM((2, 3, 3, 2, edge_rows, ch), f32),
            pltpu.VMEM((2 * (rows + 2), cols + 16, lanes), f32),
            pltpu.VMEM((2, frames + 2, rows + 2, colsp, 3 * lanes), bf16),
            pltpu.VMEM((2, 2 * rows * colsp, ch), f32),
            pltpu.SemaphoreType.DMA((2,)),
            pltpu.SemaphoreType.DMA((2, 27)),
            pltpu.SemaphoreType.DMA((2, 27)),
        ],
        compiler_params=pltpu.CompilerParams(
            collective_id=0, has_side_effects=True, vmem_limit_bytes=56 * 1024 * 1024
        ),
        name="residual_block",
    )(
        features,
        gain_first.reshape(1, ch),
        bias_first.reshape(1, ch),
        gain_second.reshape(1, ch),
        bias_second.reshape(1, ch),
        kernel_first.reshape(27, ch, ch),
        kernel_second.reshape(27, ch, ch),
    )


def solution(mesh):
    placed = (P("ta", "gy", "gx", None), P(), P(), P(), P(), P(), P())
    return jax.shard_map(
        local, mesh=mesh, in_specs=placed, out_specs=P("ta", "gy", "gx", None), check_vma=False
    )
```

time: 31 us -> 30.9 us (level)
  no operation moved by 1% of the time
where the time goes in v1:
time: 30.9 us; the launch traced here: 30.7 us
  Pallas kernels  26.8 us (87%)
  local copies, waits for them, and re-layouts  3.9 us (13%)
    pallas_call x1, Pallas kernels, local(): pl.pallas_call(block_kernel, out_shape=jax.ShapeDtypeStruct(features.shap...  26.8 us
    pallas_call x1, local copies, waits for them, and re-layouts, local(): pl.pallas_call(block_kernel, out_shape=jax.ShapeDtypeStruct(features.shap...  1.95 us
    unnamed x1, local copies, waits for them, and re-layouts  1.95 us

profile of v1, /device:TPU:5, one launch (start us, length us, event | category | flops | bytes accessed | tf_op | source)
XLA Modules:
  0.0 30.7 jit_solution(16703367018725651534)
XLA Ops:
  0.0 1.9 %copy.8.feat = bf16[4,2,104,192]{3,2,1,0:T(8,128)(2,1)} copy(bf16[4,2,104,192]{2,3,1,0:T(8,128)(2,1)} %param.7) | data formatting | bytes 638976 | tf_op args[0]
  1.9 26.8 %residual_block.1 = bf16[4,2,104,192]{3,2,1,0:T(8,128)(2,1)} custom-call(bf16[4,2,104,192]{3,2,1,0:T(8,128)(2,1)} %copy.8.feat, f32[1,192]{1,0:T(1,128)} %bitcast.8, f32[1,192]{1,0:T(1,128)} %bitcast.9, f32[1,192]{1,0:T(1,128)} %bitcast.10, f32[1,192]{1,0:T(1,128)} %bitcast.11, bf16[27,192,192]{2,1,0:T(8,128)(2,1)} %bitcast.6, bf16[27,192,192]{2,1,0:T(8,128)(2,1)} %bitcast.7), custom_call_target="tpu_custom_call" | custom-call | tf_op jit(solution)/shard_map/residual_block/pallas_call | solution.py:261
  28.7 2.0 %copy.9 = bf16[4,2,104,192]{2,3,1,0:T(8,128)(2,1)} copy(bf16[4,2,104,192]{3,2,1,0:T(8,128)(2,1)} %residual_block.1) | data formatting | bytes 638976 | tf_op jit(solution)/shard_map/residual_block/pallas_call | solution.py:261

commit v2 on v1

--- a/solution.py
+++ b/solution.py
@@ -28,7 +28,7 @@
     weights, act, edges, main_in, row_in, edge_in, line, cols3, acc,
     w_sem, send_sem, recv_sem,
 ):
-    rows, cols, ch = feat.shape[1:]
+    rows, ch, cols = feat.shape[1:]
     colsp = acc.shape[1] // (2 * rows)
     lanes = line.shape[-1]
     ta, gy, gx = (lax.axis_index(a) for a in ("ta", "gy", "gx"))
@@ -197,14 +197,14 @@
         frame = 0 if half == EARLY else 2
         for f in range(2):
             for row in range(rows):
-                value = cells(half, f, row) + bias2[...] + feat[frame + f, row].astype(jnp.float32)
+                value = (cells(half, f, row) + bias2[...]).T + feat[frame + f, row].astype(jnp.float32)
                 out[frame + f, row] = value.astype(jnp.bfloat16)
 
     def first(half):
         frame = 0 if half == EARLY else 2
         for row in range(rows):
             keep(0, half, row, [
-                activate(feat[frame + f, row].astype(jnp.float32), gain1[...]) for f in range(2)
+                activate(feat[frame + f, row].astype(jnp.float32).T, gain1[...]) for f in range(2)
             ])
 
     edges[...] = jnp.zeros_like(edges)
@@ -258,9 +258,9 @@
     hbm = pl.BlockSpec(memory_space=pl.ANY)
     edge_rows = -(-2 * rows // 8) * 8
     bf16, f32 = jnp.bfloat16, jnp.float32
-    return pl.pallas_call(
+    result = pl.pallas_call(
         block_kernel,
-        out_shape=jax.ShapeDtypeStruct(features.shape, bf16),
+        out_shape=jax.ShapeDtypeStruct((frames, rows, ch, cols), bf16),
         in_specs=[vmem] * 5 + [hbm] * 2,
         out_specs=vmem,
         scratch_shapes=[
@@ -282,7 +282,7 @@
         ),
         name="residual_block",
     )(
-        features,
+        jnp.swapaxes(features, 2, 3),
         gain_first.reshape(1, ch),
         bias_first.reshape(1, ch),
         gain_second.reshape(1, ch),
@@ -290,6 +290,7 @@
         kernel_first.reshape(27, ch, ch),
         kernel_second.reshape(27, ch, ch),
     )
+    return jnp.swapaxes(result, 2, 3)
 
 
 def solution(mesh):

time: 30.9 us -> 28.8 us (0.932)
  local copies, waits for them, and re-layouts: 3.9 us -> 1.77 us
    pallas_call x1 -> x0, local copies, waits for them, and re-layouts: 1.95 us -> none  [local(): pl.pallas_call(block_kernel, out_shape=jax.ShapeDtypeStruct(features.shap...]
where the time goes in v2:
time: 28.8 us; the launch traced here: 28.6 us
  Pallas kernels  26.9 us (93%)
  local copies, waits for them, and re-layouts  1.77 us (6%)
    pallas_call x1, Pallas kernels, local(): pl.pallas_call(block_kernel, out_shape=jax.ShapeDtypeStruct((frames, rows...  26.9 us
    unnamed x1, local copies, waits for them, and re-layouts  1.77 us

profile of v2, /device:TPU:5, one launch (start us, length us, event | category | flops | bytes accessed | tf_op | source)
XLA Modules:
  0.0 28.6 jit_solution(17279488728185174762)
XLA Ops:
  0.0 26.9 %residual_block.1 = bf16[4,2,192,104]{3,2,1,0:T(8,128)(2,1)} custom-call(bf16[4,2,192,104]{3,2,1,0:T(8,128)(2,1)} %bitcast.11, f32[1,192]{1,0:T(1,128)} %bitcast.12, f32[1,192]{1,0:T(1,128)} %bitcast.13, f32[1,192]{1,0:T(1,128)} %bitcast.14, f32[1,192]{1,0:T(1,128)} %bitcast.15, bf16[27,192,192]{2,1,0:T(8,128)(2,1)} %bitcast.8, bf16[27,192,192]{2,1,0:T(8,128)(2,1)} %bitcast.9), custom_call_target="tpu_custom_call" | custom-call | tf_op jit(solution)/shard_map/residual_block/pallas_call | solution.py:261
  26.9 1.8 %copy.9 = bf16[4,2,104,192]{2,3,1,0:T(8,128)(2,1)} copy(bf16[4,2,104,192]{2,3,1,0:T(8,128)(2,1)} %bitcast.10) | data formatting | bytes 638976

commit v3 on v2

--- a/solution.py
+++ b/solution.py
@@ -14,7 +14,7 @@
 
 
 def moves_of(kind):
-    return [m for m in MOVES if kind == PAST or m != (0, 0)]
+    return [m for m in MOVES if (kind == PAST) == (m == (0, 0))]
 
 
 def activate(field, gain):
@@ -25,7 +25,7 @@
 
 def block_kernel(
     feat, gain1, bias1, gain2, bias2, k1, k2, out,
-    weights, act, edges, main_in, row_in, edge_in, line, cols3, acc,
+    weights, act, edges, main_out, main_in, row_in, edge_in, line, cols3, acc,
     w_sem, send_sem, recv_sem,
 ):
     rows, ch, cols = feat.shape[1:]
@@ -35,12 +35,9 @@
     n_ta, n_gy, n_gx = (lax.axis_size(a) for a in ("ta", "gy", "gx"))
 
     def inside(kind, dy, dx, sign):
-        relayed = kind == PAST and dy != 0 and dx == 0
-        t = ta + sign * (1 if kind == PAST and not relayed else 0)
+        t = ta + sign * (1 if kind == PAST else 0)
         y, x = gy + sign * dy, gx + sign * dx
         ok = (t >= 0) & (t < n_ta) & (y >= 0) & (y < n_gy) & (x >= 0) & (x < n_gx)
-        if relayed:
-            ok = ok & (ta > 0)
         return ok, {"ta": t, "gy": y, "gx": x}
 
     w_copies = [
@@ -54,8 +51,6 @@
     expected = jnp.int32(0)
     for kind in (LATE, PAST):
         for dy, dx in moves_of(kind):
-            if kind == PAST and dx == 0 and dy != 0:
-                continue
             ok, source = inside(kind, dy, dx, -1)
 
             @pl.when(ok)
@@ -78,13 +73,9 @@
         if dx:
             src = edges.at[layer, half, (dx + 1) // 2]
         elif dy:
-            edge_row = rows - 1 if dy > 0 else 0
-            if kind == PAST:
-                src = main_in.at[layer, :, edge_row]
-            else:
-                src = act.at[layer, half, :, edge_row]
+            src = act.at[layer, half, :, rows - 1 if dy > 0 else 0]
         else:
-            src = act.at[layer, LATE]
+            src = main_out.at[layer]
         number = kind * 9 + (dy + 1) * 3 + dx + 1
         ok, target = inside(kind, dy, dx, 1)
         return ok, pltpu.make_async_remote_copy(
@@ -101,13 +92,8 @@
             ok, copy = copy_of(layer, kind, dy, dx)
             pl.when(ok)(copy.start)
 
-    def send_late(layer):
-        send(layer, [(LATE, -1, 0), (LATE, 1, 0)])
-        send(layer, [(kind, *m) for kind in (LATE, PAST) for m in MOVES if m[1]])
-        send(layer, [(PAST, 0, 0)])
-
-    def send_early(layer):
-        send(layer, [(EARLY, *m) for m in sorted(moves_of(EARLY), key=lambda m: (m[1] != 0, m))])
+    def send_rim(layer, half):
+        send(layer, [(half, *m) for m in sorted(moves_of(half), key=lambda m: (m[1] != 0, m))])
 
     def receive(layer, kind, moves):
         for dy, dx in moves:
@@ -119,11 +105,6 @@
             @pl.when(jnp.logical_not(ok))
             def _():
                 place[...] = jnp.zeros_like(place)
-
-    def receive_past(layer):
-        receive(layer, PAST, [(0, 0)])
-        send(layer, [(PAST, -1, 0), (PAST, 1, 0)])
-        receive(layer, PAST, [m for m in moves_of(PAST) if m != (0, 0)])
 
     def keep(layer, half, row, values):
         for f, value in enumerate(values):
@@ -137,7 +118,7 @@
         act[layer, half, 2, row] = tails.astype(jnp.bfloat16)
 
     def spread(layer, kind):
-        base = {LATE: 4, EARLY: 2, PAST: 0}[kind]
+        base = 4 if kind == LATE else 2
         for row in range(-1, rows + 1):
             if row < 0 or row >= rows:
                 dy = 1 if row < 0 else -1
@@ -145,7 +126,7 @@
                 edge_row = rows - 1 if row < 0 else 0
             else:
                 dy = 0
-                source = main_in.at[layer, :, row] if kind == PAST else act.at[layer, kind, :, row]
+                source = act.at[layer, kind, :, row]
                 edge_row = row
             tails = source[2].astype(jnp.float32)
             for f in range(2):
@@ -160,26 +141,51 @@
                         slot, 7 + r : 7 + r + cols, :
                     ].astype(jnp.bfloat16)
 
-    def convolve(layer, frame, own):
-        total_at = acc.at[1 if frame else 0]
-
-        def product(p):
-            total = None
-            for q in range(3):
-                piece = cols3[layer, pl.ds(frame + p, 2), q : q + rows].reshape(-1, 3 * lanes)
-                kernel = weights[layer, pl.ds(9 * p + 3 * q, 3)].reshape(3 * lanes, ch)
-                part = jnp.dot(piece, kernel, preferred_element_type=jnp.float32)
-                total = part if total is None else total + part
-            return total
-
+    def product(layer, frame, count, p):
+        total = None
+        for q in range(3):
+            piece = cols3[layer, pl.ds(frame, count), q : q + rows].reshape(-1, 3 * lanes)
+            kernel = weights[layer, pl.ds(9 * p + 3 * q, 3)].reshape(3 * lanes, ch)
+            part = jnp.dot(piece, kernel, preferred_element_type=jnp.float32)
+            total = part if total is None else total + part
+        return total
+
+    area = rows * colsp
+
+    def convolve_late(layer, own):
         def tap(p, _):
-            total_at[...] += product(p)
+            acc[1] += product(layer, 2 + p, 2, p)
             return 0
 
         if own:
-            total_at[...] = product(2)
+            acc[1] = product(layer, 4, 2, 2)
         else:
             lax.fori_loop(0, 2, tap, 0)
+
+    def convolve_early(layer):
+        acc[0] = product(layer, 2, 2, 2)
+        acc[0, area:] += product(layer, 2, 1, 1)
+
+    def hand_on(layer):
+        acc[2] = product(layer, 4, 2, 0)
+        acc[2, :area] += product(layer, 5, 1, 1)
+        for row in range(rows):
+            values = [acc[2, pl.ds((f * rows + row) * colsp, cols)] for f in range(2)]
+            for f, value in enumerate(values):
+                main_out[layer, f, row] = value[:, 0:TILE].astype(jnp.bfloat16)
+            tails = jnp.concatenate([value[:, TILE:ch] for value in values], axis=1)
+            main_out[layer, 2, row] = tails.astype(jnp.bfloat16)
+        send(layer, [(PAST, 0, 0)])
+
+    def add_past(layer):
+        receive(layer, PAST, [(0, 0)])
+        for row in range(rows):
+            tails = main_in[layer, 2, row].astype(jnp.float32)
+            for f in range(2):
+                at = (f * rows + row) * colsp
+                acc[0, at : at + cols, 0:TILE] += main_in[layer, f, row].astype(jnp.float32)
+                tail = pltpu.roll(tails, TILE // 2, 1) if f else tails
+                acc[0, at : at + cols, TILE:ch] += tail[:, 0 : ch - TILE]
 
     def cells(half, f, row):
         at = (f * rows + row) * colsp
@@ -210,38 +216,36 @@
     edges[...] = jnp.zeros_like(edges)
     first(LATE)
     pl.semaphore_wait(barrier, expected)
-    send_late(0)
+    send_rim(0, LATE)
     first(EARLY)
-    send_early(0)
+    send_rim(0, EARLY)
     weights[:, :, ch:, :] = jnp.zeros((2, weights.shape[1], lanes - ch, ch), jnp.bfloat16)
     line[...] = jnp.zeros_like(line)
     receive(0, LATE, moves_of(LATE))
     spread(0, LATE)
     w_copies[0].wait()
-    convolve(0, 2, True)
+    hand_on(0)
     receive(0, EARLY, moves_of(EARLY))
     spread(0, EARLY)
-    convolve(0, 2, False)
+    convolve_late(0, True)
+    convolve_late(0, False)
     middle(LATE)
-    send_late(1)
-    convolve(0, 0, True)
+    send_rim(1, LATE)
+    convolve_early(0)
     w_copies[1].wait()
     receive(1, LATE, moves_of(LATE))
     spread(1, LATE)
-    convolve(1, 2, True)
-    receive_past(0)
-    spread(0, PAST)
-    convolve(0, 0, False)
+    hand_on(1)
+    add_past(0)
     middle(EARLY)
-    send_early(1)
+    send_rim(1, EARLY)
+    convolve_late(1, True)
     receive(1, EARLY, moves_of(EARLY))
     spread(1, EARLY)
-    convolve(1, 2, False)
+    convolve_late(1, False)
     finish(LATE)
-    convolve(1, 0, True)
-    receive_past(1)
-    spread(1, PAST)
-    convolve(1, 0, False)
+    convolve_early(1)
+    add_past(1)
     finish(EARLY)
     for layer in range(2):
         for kind in (LATE, EARLY, PAST):
@@ -268,11 +272,12 @@
             pltpu.VMEM((2, 2, 3, rows, cols, TILE), bf16),
             pltpu.VMEM((2, 2, 2, edge_rows, ch), f32),
             pltpu.VMEM((2, 3, rows, cols, TILE), bf16),
-            pltpu.VMEM((2, 3, 2, 3, cols, TILE), bf16),
-            pltpu.VMEM((2, 3, 3, 2, edge_rows, ch), f32),
+            pltpu.VMEM((2, 3, rows, cols, TILE), bf16),
+            pltpu.VMEM((2, 2, 2, 3, cols, TILE), bf16),
+            pltpu.VMEM((2, 2, 3, 2, edge_rows, ch), f32),
             pltpu.VMEM((2 * (rows + 2), cols + 16, lanes), f32),
             pltpu.VMEM((2, frames + 2, rows + 2, colsp, 3 * lanes), bf16),
-            pltpu.VMEM((2, 2 * rows * colsp, ch), f32),
+            pltpu.VMEM((3, 2 * rows * colsp, ch), f32),
             pltpu.SemaphoreType.DMA((2,)),
             pltpu.SemaphoreType.DMA((2, 27)),
             pltpu.SemaphoreType.DMA((2, 27)),

time: 28.8 us -> 26.4 us (0.917)
  the two profiles are of different devices: /device:TPU:5 before, /device:TPU:0 now
where the time goes in v3:
time: 26.4 us; the launch traced here: 26.3 us
  Pallas kernels  24.5 us (93%)
  local copies, waits for them, and re-layouts  1.77 us (7%)
    pallas_call x1, Pallas kernels, local(): pl.pallas_call(block_kernel, out_shape=jax.ShapeDtypeStruct((frames, rows...  24.5 us
    unnamed x1, local copies, waits for them, and re-layouts  1.77 us

profile of v3, /device:TPU:0, one launch (start us, length us, event | category | flops | bytes accessed | tf_op | source)
XLA Modules:
  0.0 26.3 jit_solution(15175102908189522734)
XLA Ops:
  0.0 24.5 %residual_block.1 = bf16[4,2,192,104]{3,2,1,0:T(8,128)(2,1)} custom-call(bf16[4,2,192,104]{3,2,1,0:T(8,128)(2,1)} %bitcast.11, f32[1,192]{1,0:T(1,128)} %bitcast.12, f32[1,192]{1,0:T(1,128)} %bitcast.13, f32[1,192]{1,0:T(1,128)} %bitcast.14, f32[1,192]{1,0:T(1,128)} %bitcast.15, bf16[27,192,192]{2,1,0:T(8,128)(2,1)} %bitcast.8, bf16[27,192,192]{2,1,0:T(8,128)(2,1)} %bitcast.9), custom_call_target="tpu_custom_call" | custom-call | tf_op jit(solution)/shard_map/residual_block/pallas_call | solution.py:265
  24.5 1.8 %copy.9 = bf16[4,2,104,192]{2,3,1,0:T(8,128)(2,1)} copy(bf16[4,2,104,192]{2,3,1,0:T(8,128)(2,1)} %bitcast.10) | data formatting | bytes 638976

commit v4 on v3

--- a/solution.py
+++ b/solution.py
@@ -153,14 +153,10 @@
     area = rows * colsp
 
     def convolve_late(layer, own):
-        def tap(p, _):
-            acc[1] += product(layer, 2 + p, 2, p)
-            return 0
-
         if own:
             acc[1] = product(layer, 4, 2, 2)
         else:
-            lax.fori_loop(0, 2, tap, 0)
+            acc[1] += product(layer, 2, 2, 0) + product(layer, 3, 2, 1)
 
     def convolve_early(layer):
         acc[0] = product(layer, 2, 2, 2)

time: 26.4 us -> 26 us (0.985)
  Pallas kernels: 24.5 us -> 24.1 us
    pallas_call x1, Pallas kernels: 24.5 us -> 24.1 us  [local(): pl.pallas_call(block_kernel, out_shape=jax.ShapeDtypeStruct((frames, rows...]
where the time goes in v4:
time: 26 us; the launch traced here: 25.9 us
  Pallas kernels  24.1 us (93%)
  local copies, waits for them, and re-layouts  1.77 us (7%)
    pallas_call x1, Pallas kernels, local(): pl.pallas_call(block_kernel, out_shape=jax.ShapeDtypeStruct((frames, rows...  24.1 us
    unnamed x1, local copies, waits for them, and re-layouts  1.77 us

profile of v4, /device:TPU:0, one launch (start us, length us, event | category | flops | bytes accessed | tf_op | source)
XLA Modules:
  0.0 25.9 jit_solution(2650408647411177961)
XLA Ops:
  0.0 24.1 %residual_block.1 = bf16[4,2,192,104]{3,2,1,0:T(8,128)(2,1)} custom-call(bf16[4,2,192,104]{3,2,1,0:T(8,128)(2,1)} %bitcast.11, f32[1,192]{1,0:T(1,128)} %bitcast.12, f32[1,192]{1,0:T(1,128)} %bitcast.13, f32[1,192]{1,0:T(1,128)} %bitcast.14, f32[1,192]{1,0:T(1,128)} %bitcast.15, bf16[27,192,192]{2,1,0:T(8,128)(2,1)} %bitcast.8, bf16[27,192,192]{2,1,0:T(8,128)(2,1)} %bitcast.9), custom_call_target="tpu_custom_call" | custom-call | tf_op jit(solution)/shard_map/residual_block/pallas_call | solution.py:261
  24.1 1.8 %copy.9 = bf16[4,2,104,192]{2,3,1,0:T(8,128)(2,1)} copy(bf16[4,2,104,192]{2,3,1,0:T(8,128)(2,1)} %bitcast.10) | data formatting | bytes 638976
